TPU v7x, 32 devices: a whole 2x2x4 slice. The times are simulated.
32 devices in a mesh: sp: 16 (over z, x, core), dp: 2 (over y).
Axes of the slice: x: 2, y: 2, z: 4, core: 2. Of those that a mesh axis runs over, the one named last changes fastest.
Arguments:
- queries: bfloat16 [1536, 24, 128], P(('dp', 'sp')), parts along dimension 0, may hold values from -12 to 12
- keys: bfloat16 [1536, 24, 128], P(('dp', 'sp')), parts along dimension 0, may hold values from -6 to 6
- values: bfloat16 [1536, 24, 128], P(('dp', 'sp')), parts along dimension 0, may hold values from -6 to 6
Outputs:
- attended: bfloat16 [1536, 3072], P(('dp', 'sp')), parts along dimension 0
There are 2 independent parts, one for each index of `dp`. A program takes and returns all parts, laid end to end along the dimension named above; each array names one. Nothing has to cross between parts.
All inputs are finite; a program needn't handle non-finite values.
Results may differ from a plain program's by a relative error of at most 0.0049.
Values may be sent and summed in bfloat16 or wider, within the bound.
No kernel may reach another device: no remote copies, remote signals or barrier semaphores. Data moves between devices by JAX's collectives and lax.ppermute only.
A program may use at most 64 MiB of HBM per device.

v0:
```python
import functools
import math

import jax
import jax.numpy as jnp
from jax import lax
from jax.experimental import pallas as pl
from jax.experimental.pallas import tpu as pltpu
from jax.sharding import PartitionSpec as P


CORES = 2
GROUPS = 4

VMEM = pltpu.MemorySpace.VMEM
SMEM = pltpu.MemorySpace.SMEM
PARAMS = pltpu.CompilerParams(vmem_limit_bytes=24 << 20)


def local(count):
    return [pl.BlockSpec(memory_space=VMEM)] * count


def scalar():
    return [pl.BlockSpec(memory_space=SMEM)]


def pack_kernel(group_ref, q_ref, k_ref, v_ref, *refs, groups):
    near, far, wide = refs[:groups], refs[groups : 2 * groups], refs[2 * groups]
    tokens, heads, width = q_ref.shape
    per_group = heads // groups
    group = group_ref[0]
    for part, ref in enumerate((k_ref, v_ref, q_ref)):
        wide[part] = ref[...].reshape(tokens * heads, width).astype(jnp.float32)
        for mask in range(groups):
            first = (group ^ mask) * per_group
            for head in range(per_group):
                rows = wide[part, pl.ds(first + head, tokens, stride=heads), :].astype(q_ref.dtype)
                near[mask][part, head] = rows
                if part < 2:
                    far[mask][part, head] = rows


def pack(group, queries, keys, values, groups):
    tokens, heads, width = queries.shape
    near = pltpu.VMEM((3, heads // groups, tokens, width), queries.dtype)
    far = pltpu.VMEM((2, heads // groups, tokens, width), queries.dtype)
    outs = pl.pallas_call(
        functools.partial(pack_kernel, groups=groups),
        in_specs=scalar() + local(3),
        out_specs=local(2 * groups),
        out_shape=[near] * groups + [far] * groups,
        scratch_shapes=[pltpu.VMEM((3, tokens * heads, width), jnp.float32)],
        compiler_params=PARAMS,
    )(group, queries, keys, values)
    return outs[:groups], outs[groups:]


def block(head_q, pieces, head, scale):
    head_k = jnp.concatenate([piece[0, head] for piece in pieces])
    head_v = jnp.concatenate([piece[1, head] for piece in pieces])
    scores = lax.dot_general(head_q, head_k, (((1,), (1,)), ((), ())), preferred_element_type=jnp.float32)
    largest = jnp.max(scores, axis=-1, keepdims=True)
    weights = jnp.exp2((scores - largest) * scale)
    total = jnp.sum(weights, axis=-1, keepdims=True)
    summed = jnp.dot(weights.astype(head_v.dtype), head_v, preferred_element_type=jnp.float32)
    return largest, total, summed


def first_kernel(*refs, groups, count, scale):
    pieces, (q_out, largest_out, total_out, summed_out) = refs[:count], refs[count:]
    for head in range(q_out.shape[0]):
        head_q = jnp.concatenate([piece[2, head] for piece in pieces[:groups]])
        q_out[head] = head_q
        largest, total, summed = block(head_q, pieces, head, scale)
        largest_out[head] = largest
        total_out[head] = total
        summed_out[head] = summed


def attend_first(pieces, groups, scale):
    _, per_group, tokens, width = pieces[0].shape
    rows = groups * tokens
    return pl.pallas_call(
        functools.partial(first_kernel, groups=groups, count=len(pieces), scale=scale),
        in_specs=local(len(pieces)),
        out_specs=local(4),
        out_shape=[
            pltpu.VMEM((per_group, rows, width), pieces[0].dtype),
            pltpu.VMEM((per_group, rows, 1), jnp.float32),
            pltpu.VMEM((per_group, rows, 1), jnp.float32),
            pltpu.VMEM((per_group, rows, width), jnp.float32),
        ],
        compiler_params=PARAMS,
    )(*map(inside, pieces))


def last_kernel(q_ref, largest_ref, total_ref, summed_ref, *refs, count, scale):
    pieces, outs = refs[:count], refs[count:]
    per_group, tokens, width = pieces[0].shape[1:]
    for head in range(per_group):
        largest, total, summed = block(q_ref[head], pieces, head, scale)
        before = largest_ref[head]
        top = jnp.maximum(largest, before)
        now, then = jnp.exp2((largest - top) * scale), jnp.exp2((before - top) * scale)
        inverse = 1.0 / (total * now + total_ref[head] * then)
        result = summed * (now * inverse) + summed_ref[head] * (then * inverse)
        result = result.astype(pieces[0].dtype)
        for mask, out in enumerate(outs):
            out[:, head * width : (head + 1) * width] = result[mask * tokens : (mask + 1) * tokens]


def attend_last(state, pieces, groups, scale):
    _, per_group, tokens, width = pieces[0].shape
    out = pltpu.VMEM((tokens, per_group * width), pieces[0].dtype)
    return pl.pallas_call(
        functools.partial(last_kernel, count=len(pieces), scale=scale),
        in_specs=local(4 + len(pieces)),
        out_specs=local(groups),
        out_shape=[out] * groups,
        compiler_params=PARAMS,
    )(*map(inside, state), *map(inside, pieces))


def unpack_kernel(group_ref, *refs):
    pieces, out_ref = refs[:-1], refs[-1]
    feat = pieces[0].shape[1]
    group = group_ref[0]
    for mask, piece in enumerate(pieces):
        first = pl.multiple_of((group ^ mask) * feat, 128)
        out_ref[:, pl.ds(first, feat)] = piece[...]


def unpack(group, pieces):
    tokens, feat = pieces[0].shape
    return pl.pallas_call(
        unpack_kernel,
        in_specs=scalar() + local(len(pieces)),
        out_specs=pl.BlockSpec(memory_space=VMEM),
        out_shape=jax.ShapeDtypeStruct((tokens, len(pieces) * feat), pieces[0].dtype),
        compiler_params=PARAMS,
    )(group, *map(inside, pieces))


def inside(x):
    return pltpu.with_memory_space_constraint(x, pltpu.MemorySpace.VMEM)


def shards(queries, keys, values):
    heads, width = queries.shape[1:]
    devices = lax.axis_size("sp")
    groups = min(GROUPS, heads & -heads, devices // CORES)
    regions = devices // (groups * CORES)
    scale = math.log2(math.e) / math.sqrt(width)
    group = (lax.axis_index("sp") // CORES % groups).astype(jnp.int32).reshape(1)

    def across(piece, mask, step):
        pairs = []
        for i in range(devices):
            region, own, core = i // (groups * CORES), i // CORES % groups, i % CORES
            pairs.append((i, (((region + step) % regions) * groups + (own ^ mask)) * CORES + core))
        return lax.ppermute(piece, "sp", pairs)

    def sibling(piece):
        pairs = [(i, i // CORES * CORES + (i + 1) % CORES) for i in range(devices)]
        return lax.ppermute(piece, "sp", pairs)

    near, far = pack(group, queries, keys, values, groups)
    far_in, far_all, near_in, near_all = [], [], [near[0]], []
    for step in range(1, regions):
        for mask in reversed(range(groups)):
            far_in.append(across(far[mask], mask, step))
    for mask in range(1, groups):
        near_in.append(across(near[mask], mask, 0))
    near_all = near_in + [sibling(far[0])] + [sibling(piece) for piece in near_in[1:]]
    state = attend_first(near_all, groups, scale)
    far_all = far_in + [sibling(piece) for piece in far_in]
    results = attend_last(state, far_all, groups, scale)
    returned = [results[0]] + [across(results[mask], mask, 0) for mask in range(1, groups)]
    return unpack(group, returned)


def solution(mesh):
    spec = P(("dp", "sp"), None, None)
    return jax.shard_map(
        shards,
        mesh=mesh,
        in_specs=(spec, spec, spec),
        out_specs=P(("dp", "sp"), None),
        check_vma=False,
    )
```

profile of v0, /device:TPU:0, one launch (start us, length us, event | category | flops | bytes accessed | tf_op | source)
XLA Modules:
  0.0 53.2 jit_solution(8967544222664762431)
XLA Ops:
  0.0 1.0 %copy-done = bf16[48,24,128]{2,1,0:T(8,128)(2,1)S(1)} copy-done((bf16[48,24,128]{2,1,0:T(8,128)(2,1)S(1)}, bf16[48,24,128]{2,1,0:T(8,128)(2,1)}, u32[]{:S(2)}) %copy-start) | copy-done | bytes 294936
  1.0 1.0 %copy-done.1 = bf16[48,24,128]{2,1,0:T(8,128)(2,1)S(1)} copy-done((bf16[48,24,128]{2,1,0:T(8,128)(2,1)S(1)}, bf16[48,24,128]{2,1,0:T(8,128)(2,1)}, u32[]{:S(2)}) %copy-start.1) | copy-done | bytes 294936
  1.9 1.0 %copy-done.2 = bf16[48,24,128]{2,1,0:T(8,128)(2,1)S(1)} copy-done((bf16[48,24,128]{2,1,0:T(8,128)(2,1)S(1)}, bf16[48,24,128]{2,1,0:T(8,128)(2,1)}, u32[]{:S(2)}) %copy-start.2) | copy-done | bytes 294936
  2.9 0.4 shard_map.37
  3.3 0.6 %collective-permute-start.3 = (bf16[2,6,48,128]{3,2,1,0:T(8,128)(2,1)S(1)}, bf16[2,6,48,128]{3,2,1,0:T(8,128)(2,1)S(1)}, u32[]{:S(2)}, u32[]{:S(2)}) collective-permute-start(bf16[2,6,48,128]{3,2,1,0:T(8,128)(2,1)S(1)} %get-tuple-element.25), channel_id=1, source_target_pairs={{0,2},{2,0},{4,6},{6,4},{8,10},{10,8},{12,14},{14,12},{16,18},{18,... | collective-permute-start | bytes 442376 | tf_op jit(solution)/shard_map/ppermute | solution.py:166
  3.9 2.6 %collective-permute-start = (bf16[3,6,48,128]{3,2,1,0:T(8,128)(2,1)S(1)}, bf16[3,6,48,128]{3,2,1,0:T(8,128)(2,1)S(1)}, u32[]{:S(2)}, u32[]{:S(2)}) collective-permute-start(bf16[3,6,48,128]{3,2,1,0:T(8,128)(2,1)S(1)} %get-tuple-element.22), channel_id=1, source_target_pairs={{0,4},{2,6},{4,0},{6,2},{8,12},{10,14},{12,8},{14,10},{16,20},{18,... | collective-permute-start | bytes 663560 | tf_op jit(solution)/shard_map/ppermute | solution.py:162
  6.4 1.6 %collective-permute-start.1 = (bf16[3,6,48,128]{3,2,1,0:T(8,128)(2,1)S(1)}, bf16[3,6,48,128]{3,2,1,0:T(8,128)(2,1)S(1)}, u32[]{:S(2)}, u32[]{:S(2)}) collective-permute-start(bf16[3,6,48,128]{3,2,1,0:T(8,128)(2,1)S(1)} %get-tuple-element.23), channel_id=1, source_target_pairs={{0,8},{2,10},{4,12},{6,14},{8,0},{10,2},{12,4},{14,6},{16,24},{18,... | collective-permute-start | bytes 663560 | tf_op jit(solution)/shard_map/ppermute | solution.py:162
  8.0 4.9 %collective-permute-start.7 = (bf16[2,6,48,128]{3,2,1,0:T(8,128)(2,1)S(1)}, bf16[2,6,48,128]{3,2,1,0:T(8,128)(2,1)S(1)}, u32[]{:S(2)}, u32[]{:S(2)}) collective-permute-start(bf16[2,6,48,128]{3,2,1,0:T(8,128)(2,1)S(1)} %get-tuple-element.30), channel_id=1, source_target_pairs={{0,28},{2,30},{4,24},{6,26},{8,20},{10,22},{12,16},{14,18},{16,12}... | collective-permute-start | bytes 442376 | tf_op jit(solution)/shard_map/ppermute | solution.py:162
  12.9 0.0 collective-permute-done.3.refs_4_
  12.9 0.2 collective-permute-start.8
  13.2 0.0 collective-permute-done.refs_1_
  13.2 0.0 collective-permute-start.4
  13.2 1.5 %collective-permute-done.1.refs_2_ = bf16[3,6,48,128]{3,2,1,0:T(8,128)(2,1)S(1)} collective-permute-done((bf16[3,6,48,128]{3,2,1,0:T(8,128)(2,1)S(1)}, bf16[3,6,48,128]{3,2,1,0:T(8,128)(2,1)S(1)}, u32[]{:S(2)}, u32[]{:S(2)}) %collective-permute-start.1) | collective-permute-done | bytes 221216 | tf_op jit(solution)/shard_map/ppermute | solution.py:162
  14.7 0.0 collective-permute-start.5
  14.7 10.7 %collective-permute-done.7.refs_0_ = bf16[2,6,48,128]{3,2,1,0:T(8,128)(2,1)S(1)} collective-permute-done((bf16[2,6,48,128]{3,2,1,0:T(8,128)(2,1)S(1)}, bf16[2,6,48,128]{3,2,1,0:T(8,128)(2,1)S(1)}, u32[]{:S(2)}, u32[]{:S(2)}) %collective-permute-start.7) | collective-permute-done | bytes 147488 | tf_op jit(solution)/shard_map/ppermute | solution.py:162
  25.4 0.0 collective-permute-start.9
  25.4 3.2 %collective-permute-done.8.refs_1_ = bf16[2,6,48,128]{3,2,1,0:T(8,128)(2,1)S(1)} collective-permute-done((bf16[2,6,48,128]{3,2,1,0:T(8,128)(2,1)S(1)}, bf16[2,6,48,128]{3,2,1,0:T(8,128)(2,1)S(1)}, u32[]{:S(2)}, u32[]{:S(2)}) %collective-permute-start.8) | collective-permute-done | bytes 147488 | tf_op jit(solution)/shard_map/ppermute | solution.py:162
  28.7 0.6 %collective-permute-start.10 = (bf16[2,6,48,128]{3,2,1,0:T(8,128)(2,1)S(1)}, bf16[2,6,48,128]{3,2,1,0:T(8,128)(2,1)S(1)}, u32[]{:S(2)}, u32[]{:S(2)}) collective-permute-start(bf16[2,6,48,128]{3,2,1,0:T(8,128)(2,1)S(1)} %get-tuple-element.25), channel_id=1, source_target_pairs={{0,16},{2,18},{4,20},{6,22},{8,24},{10,26},{12,28},{14,30},{16,0},... | collective-permute-start | bytes 442376 | tf_op jit(solution)/shard_map/ppermute | solution.py:162
  29.3 0.0 collective-permute-done.2.refs_3_
  29.3 8.1 %collective-permute-done.9.refs_2_ = bf16[2,6,48,128]{3,2,1,0:T(8,128)(2,1)S(1)} collective-permute-done((bf16[2,6,48,128]{3,2,1,0:T(8,128)(2,1)S(1)}, bf16[2,6,48,128]{3,2,1,0:T(8,128)(2,1)S(1)}, u32[]{:S(2)}, u32[]{:S(2)}) %collective-permute-start.9) | collective-permute-done | bytes 147488 | tf_op jit(solution)/shard_map/ppermute | solution.py:162
  37.4 3.1 %collective-permute-done.10.refs_3_ = bf16[2,6,48,128]{3,2,1,0:T(8,128)(2,1)S(1)} collective-permute-done((bf16[2,6,48,128]{3,2,1,0:T(8,128)(2,1)S(1)}, bf16[2,6,48,128]{3,2,1,0:T(8,128)(2,1)S(1)}, u32[]{:S(2)}, u32[]{:S(2)}) %collective-permute-start.10) | collective-permute-done | bytes 147488 | tf_op jit(solution)/shard_map/ppermute | solution.py:162
  40.4 0.0 collective-permute-start.12
  40.5 0.5 collective-permute-start.13
  41.0 0.1 collective-permute-start.14
  41.0 1.8 %shard_map.38 = (bf16[6,192,128]{2,1,0:T(8,128)(2,1)S(1)}, f32[6,192,1]{2,1,0:T(8,128)S(1)}, f32[6,192,1]{2,1,0:T(8,128)S(1)}, f32[6,192,128]{2,1,0:T(8,128)S(1)}) custom-call(bf16[3,6,48,128]{3,2,1,0:T(8,128)(2,1)S(1)} %get-tuple-element.21.refs_0_, bf16[3,6,48,128]{3,2,1,0:T(8,128)(2,1)S(1)} %collective-permute-done.refs_1_, ...), custom_call_target="tpu_custom_call" | custom-call | tf_op jit(solution)/shard_map/pallas_call | solution.py:84
  42.9 2.1 %shard_map.39 = (bf16[48,768]{1,0:T(8,128)(2,1)S(1)}, bf16[48,768]{1,0:T(8,128)(2,1)S(1)}, bf16[48,768]{1,0:T(8,128)(2,1)S(1)}, bf16[48,768]{1,0:T(8,128)(2,1)S(1)}) custom-call(bf16[6,192,128]{2,1,0:T(8,128)(2,1)S(1)} %get-tuple-element.26.q_ref, f32[6,192,1]{2,1,0:T(8,128)S(1)} %get-tuple-element.27.largest_ref, ...), custom_call_target="tpu_custom_call" | custom-call | tf_op jit(solution)/shard_map/pallas_call | solution.py:116
  45.0 0.6 %collective-permute-start.15 = (bf16[48,768]{1,0:T(8,128)(2,1)S(1)}, bf16[48,768]{1,0:T(8,128)(2,1)S(1)}, u32[]{:S(2)}, u32[]{:S(2)}) collective-permute-start(bf16[48,768]{1,0:T(8,128)(2,1)S(1)} %get-tuple-element.34), channel_id=1, source_target_pairs={{0,4},{2,6},{4,0},{6,2},{8,12},{10,14},{12,8},{14,10},{16,20},{18,... | collective-permute-start | bytes 221192 | tf_op jit(solution)/shard_map/ppermute | solution.py:162
  45.6 2.9 %collective-permute-start.17 = (bf16[48,768]{1,0:T(8,128)(2,1)S(1)}, bf16[48,768]{1,0:T(8,128)(2,1)S(1)}, u32[]{:S(2)}, u32[]{:S(2)}) collective-permute-start(bf16[48,768]{1,0:T(8,128)(2,1)S(1)} %get-tuple-element.36), channel_id=1, source_target_pairs={{0,12},{2,14},{4,8},{6,10},{8,4},{10,6},{12,0},{14,2},{16,28},{18,... | collective-permute-start | bytes 221192 | tf_op jit(solution)/shard_map/ppermute | solution.py:162
  48.5 1.1 %collective-permute-done.15.refs_1_ = bf16[48,768]{1,0:T(8,128)(2,1)S(1)} collective-permute-done((bf16[48,768]{1,0:T(8,128)(2,1)S(1)}, bf16[48,768]{1,0:T(8,128)(2,1)S(1)}, u32[]{:S(2)}, u32[]{:S(2)}) %collective-permute-start.15) | collective-permute-done | bytes 73760 | tf_op jit(solution)/shard_map/ppermute | solution.py:162
  49.7 1.0 %collective-permute-done.16.refs_2_ = bf16[48,768]{1,0:T(8,128)(2,1)S(1)} collective-permute-done((bf16[48,768]{1,0:T(8,128)(2,1)S(1)}, bf16[48,768]{1,0:T(8,128)(2,1)S(1)}, u32[]{:S(2)}, u32[]{:S(2)}) %collective-permute-start.16) | collective-permute-done | bytes 73760 | tf_op jit(solution)/shard_map/ppermute | solution.py:162
  50.6 1.8 %collective-permute-done.17.refs_3_ = bf16[48,768]{1,0:T(8,128)(2,1)S(1)} collective-permute-done((bf16[48,768]{1,0:T(8,128)(2,1)S(1)}, bf16[48,768]{1,0:T(8,128)(2,1)S(1)}, u32[]{:S(2)}, u32[]{:S(2)}) %collective-permute-start.17) | collective-permute-done | bytes 73760 | tf_op jit(solution)/shard_map/ppermute | solution.py:162
  52.4 0.7 %shard_map.40 = bf16[48,3072]{1,0:T(8,128)(2,1)} custom-call(s32[1]{0:T(128)} %bitcast.group_ref, bf16[48,768]{1,0:T(8,128)(2,1)S(1)} %get-tuple-element.33.refs_0_, bf16[48,768]{1,0:T(8,128)(2,1)S(1)} %collective-permute-done.15.refs_1_, bf16[48,768]{1,0:T(8,128)(2,1)S(1)} %collective-permute-done.16.refs_2_, ...), custom_call_target="tpu_custom_call" | custom-call | tf_op jit(solution)/shard_map/pallas_call | solution.py:136
  (14 shorter events, 0.0 us)
Async XLA Ops:
  0.0 1.0 %copy-start = (bf16[48,24,128]{2,1,0:T(8,128)(2,1)S(1)}, bf16[48,24,128]{2,1,0:T(8,128)(2,1)}, u32[]{:S(2)}) copy-start(bf16[48,24,128]{2,1,0:T(8,128)(2,1)} %q_ref.1) | copy-start | bytes 884740
  1.0 1.0 %copy-start.1 = (bf16[48,24,128]{2,1,0:T(8,128)(2,1)S(1)}, bf16[48,24,128]{2,1,0:T(8,128)(2,1)}, u32[]{:S(2)}) copy-start(bf16[48,24,128]{2,1,0:T(8,128)(2,1)} %k_ref.1) | copy-start | bytes 884740
  1.9 1.0 %copy-start.2 = (bf16[48,24,128]{2,1,0:T(8,128)(2,1)S(1)}, bf16[48,24,128]{2,1,0:T(8,128)(2,1)}, u32[]{:S(2)}) copy-start(bf16[48,24,128]{2,1,0:T(8,128)(2,1)} %v_ref.1) | copy-start | bytes 884740
  3.3 9.6 %collective-permute-start.3 = (bf16[2,6,48,128]{3,2,1,0:T(8,128)(2,1)S(1)}, bf16[2,6,48,128]{3,2,1,0:T(8,128)(2,1)S(1)}, u32[]{:S(2)}, u32[]{:S(2)}) collective-permute-start(bf16[2,6,48,128]{3,2,1,0:T(8,128)(2,1)S(1)} %get-tuple-element.25), channel_id=1, source_target_pairs={{0,2},{2,0},{4,6},{6,4},{8,10},{10,8},{12,14},{14,12},{16,18},{18,... | collective-permute-start | bytes 442376 | tf_op jit(solution)/shard_map/ppermute | solution.py:166
  3.9 9.3 %collective-permute-start = (bf16[3,6,48,128]{3,2,1,0:T(8,128)(2,1)S(1)}, bf16[3,6,48,128]{3,2,1,0:T(8,128)(2,1)S(1)}, u32[]{:S(2)}, u32[]{:S(2)}) collective-permute-start(bf16[3,6,48,128]{3,2,1,0:T(8,128)(2,1)S(1)} %get-tuple-element.22), channel_id=1, source_target_pairs={{0,4},{2,6},{4,0},{6,2},{8,12},{10,14},{12,8},{14,10},{16,20},{18,... | collective-permute-start | bytes 663560 | tf_op jit(solution)/shard_map/ppermute | solution.py:162
  6.4 8.3 %collective-permute-start.1 = (bf16[3,6,48,128]{3,2,1,0:T(8,128)(2,1)S(1)}, bf16[3,6,48,128]{3,2,1,0:T(8,128)(2,1)S(1)}, u32[]{:S(2)}, u32[]{:S(2)}) collective-permute-start(bf16[3,6,48,128]{3,2,1,0:T(8,128)(2,1)S(1)} %get-tuple-element.23), channel_id=1, source_target_pairs={{0,8},{2,10},{4,12},{6,14},{8,0},{10,2},{12,4},{14,6},{16,24},{18,... | collective-permute-start | bytes 663560 | tf_op jit(solution)/shard_map/ppermute | solution.py:162
  8.0 21.3 %collective-permute-start.2 = (bf16[3,6,48,128]{3,2,1,0:T(8,128)(2,1)S(1)}, bf16[3,6,48,128]{3,2,1,0:T(8,128)(2,1)S(1)}, u32[]{:S(2)}, u32[]{:S(2)}) collective-permute-start(bf16[3,6,48,128]{3,2,1,0:T(8,128)(2,1)S(1)} %get-tuple-element.24), channel_id=1, source_target_pairs={{0,12},{2,14},{4,8},{6,10},{8,4},{10,6},{12,0},{14,2},{16,28},{18,... | collective-permute-start | bytes 663560 | tf_op jit(solution)/shard_map/ppermute | solution.py:162
  8.0 17.4 %collective-permute-start.7 = (bf16[2,6,48,128]{3,2,1,0:T(8,128)(2,1)S(1)}, bf16[2,6,48,128]{3,2,1,0:T(8,128)(2,1)S(1)}, u32[]{:S(2)}, u32[]{:S(2)}) collective-permute-start(bf16[2,6,48,128]{3,2,1,0:T(8,128)(2,1)S(1)} %get-tuple-element.30), channel_id=1, source_target_pairs={{0,28},{2,30},{4,24},{6,26},{8,20},{10,22},{12,16},{14,18},{16,12}... | collective-permute-start | bytes 442376 | tf_op jit(solution)/shard_map/ppermute | solution.py:162
  12.9 15.7 %collective-permute-start.8 = (bf16[2,6,48,128]{3,2,1,0:T(8,128)(2,1)S(1)}, bf16[2,6,48,128]{3,2,1,0:T(8,128)(2,1)S(1)}, u32[]{:S(2)}, u32[]{:S(2)}) collective-permute-start(bf16[2,6,48,128]{3,2,1,0:T(8,128)(2,1)S(1)} %get-tuple-element.31), channel_id=1, source_target_pairs={{0,24},{2,26},{4,28},{6,30},{8,16},{10,18},{12,20},{14,22},{16,8},... | collective-permute-start | bytes 442376 | tf_op jit(solution)/shard_map/ppermute | solution.py:162
  13.2 27.3 %collective-permute-start.4 = (bf16[3,6,48,128]{3,2,1,0:T(8,128)(2,1)S(1)}, bf16[3,6,48,128]{3,2,1,0:T(8,128)(2,1)S(1)}, u32[]{:S(2)}, u32[]{:S(2)}) collective-permute-start(bf16[3,6,48,128]{3,2,1,0:T(8,128)(2,1)S(1)} %collective-permute-done.refs_1_), channel_id=1, source_target_pairs={{0,2},{2,0},{4,6},{6,4},{8,10},{10,8},{12,14},{14,12},{16,18},{18,... | collective-permute-start | bytes 663560 | tf_op jit(solution)/shard_map/ppermute | solution.py:166
  14.7 26.3 %collective-permute-start.5 = (bf16[3,6,48,128]{3,2,1,0:T(8,128)(2,1)S(1)}, bf16[3,6,48,128]{3,2,1,0:T(8,128)(2,1)S(1)}, u32[]{:S(2)}, u32[]{:S(2)}) collective-permute-start(bf16[3,6,48,128]{3,2,1,0:T(8,128)(2,1)S(1)} %collective-permute-done.1.refs_2_), channel_id=1, source_target_pairs={{0,2},{2,0},{4,6},{6,4},{8,10},{10,8},{12,14},{14,12},{16,18},{18,... | collective-permute-start | bytes 663560 | tf_op jit(solution)/shard_map/ppermute | solution.py:166
  25.4 11.9 %collective-permute-start.9 = (bf16[2,6,48,128]{3,2,1,0:T(8,128)(2,1)S(1)}, bf16[2,6,48,128]{3,2,1,0:T(8,128)(2,1)S(1)}, u32[]{:S(2)}, u32[]{:S(2)}) collective-permute-start(bf16[2,6,48,128]{3,2,1,0:T(8,128)(2,1)S(1)} %get-tuple-element.32), channel_id=1, source_target_pairs={{0,20},{2,22},{4,16},{6,18},{8,28},{10,30},{12,24},{14,26},{16,4},... | collective-permute-start | bytes 442376 | tf_op jit(solution)/shard_map/ppermute | solution.py:162
  28.7 11.8 %collective-permute-start.10 = (bf16[2,6,48,128]{3,2,1,0:T(8,128)(2,1)S(1)}, bf16[2,6,48,128]{3,2,1,0:T(8,128)(2,1)S(1)}, u32[]{:S(2)}, u32[]{:S(2)}) collective-permute-start(bf16[2,6,48,128]{3,2,1,0:T(8,128)(2,1)S(1)} %get-tuple-element.25), channel_id=1, source_target_pairs={{0,16},{2,18},{4,20},{6,22},{8,24},{10,26},{12,28},{14,30},{16,0},... | collective-permute-start | bytes 442376 | tf_op jit(solution)/shard_map/ppermute | solution.py:162
  29.3 11.7 %collective-permute-start.6 = (bf16[3,6,48,128]{3,2,1,0:T(8,128)(2,1)S(1)}, bf16[3,6,48,128]{3,2,1,0:T(8,128)(2,1)S(1)}, u32[]{:S(2)}, u32[]{:S(2)}) collective-permute-start(bf16[3,6,48,128]{3,2,1,0:T(8,128)(2,1)S(1)} %collective-permute-done.2.refs_3_), channel_id=1, source_target_pairs={{0,2},{2,0},{4,6},{6,4},{8,10},{10,8},{12,14},{14,12},{16,18},{18,... | collective-permute-start | bytes 663560 | tf_op jit(solution)/shard_map/ppermute | solution.py:166
  37.4 5.5 %collective-permute-start.11 = (bf16[2,6,48,128]{3,2,1,0:T(8,128)(2,1)S(1)}, bf16[2,6,48,128]{3,2,1,0:T(8,128)(2,1)S(1)}, u32[]{:S(2)}, u32[]{:S(2)}) collective-permute-start(bf16[2,6,48,128]{3,2,1,0:T(8,128)(2,1)S(1)} %collective-permute-done.7.refs_0_), channel_id=1, source_target_pairs={{0,2},{2,0},{4,6},{6,4},{8,10},{10,8},{12,14},{14,12},{16,18},{18,... | collective-permute-start | bytes 442376 | tf_op jit(solution)/shard_map/ppermute | solution.py:166
  40.4 2.4 %collective-permute-start.12 = (bf16[2,6,48,128]{3,2,1,0:T(8,128)(2,1)S(1)}, bf16[2,6,48,128]{3,2,1,0:T(8,128)(2,1)S(1)}, u32[]{:S(2)}, u32[]{:S(2)}) collective-permute-start(bf16[2,6,48,128]{3,2,1,0:T(8,128)(2,1)S(1)} %collective-permute-done.8.refs_1_), channel_id=1, source_target_pairs={{0,2},{2,0},{4,6},{6,4},{8,10},{10,8},{12,14},{14,12},{16,18},{18,... | collective-permute-start | bytes 442376 | tf_op jit(solution)/shard_map/ppermute | solution.py:166
  40.5 2.4 %collective-permute-start.13 = (bf16[2,6,48,128]{3,2,1,0:T(8,128)(2,1)S(1)}, bf16[2,6,48,128]{3,2,1,0:T(8,128)(2,1)S(1)}, u32[]{:S(2)}, u32[]{:S(2)}) collective-permute-start(bf16[2,6,48,128]{3,2,1,0:T(8,128)(2,1)S(1)} %collective-permute-done.9.refs_2_), channel_id=1, source_target_pairs={{0,2},{2,0},{4,6},{6,4},{8,10},{10,8},{12,14},{14,12},{16,18},{18,... | collective-permute-start | bytes 442376 | tf_op jit(solution)/shard_map/ppermute | solution.py:166
  41.0 1.9 %collective-permute-start.14 = (bf16[2,6,48,128]{3,2,1,0:T(8,128)(2,1)S(1)}, bf16[2,6,48,128]{3,2,1,0:T(8,128)(2,1)S(1)}, u32[]{:S(2)}, u32[]{:S(2)}) collective-permute-start(bf16[2,6,48,128]{3,2,1,0:T(8,128)(2,1)S(1)} %collective-permute-done.10.refs_3_), channel_id=1, source_target_pairs={{0,2},{2,0},{4,6},{6,4},{8,10},{10,8},{12,14},{14,12},{16,18},{18,... | collective-permute-start | bytes 442376 | tf_op jit(solution)/shard_map/ppermute | solution.py:166
  45.0 4.7 %collective-permute-start.15 = (bf16[48,768]{1,0:T(8,128)(2,1)S(1)}, bf16[48,768]{1,0:T(8,128)(2,1)S(1)}, u32[]{:S(2)}, u32[]{:S(2)}) collective-permute-start(bf16[48,768]{1,0:T(8,128)(2,1)S(1)} %get-tuple-element.34), channel_id=1, source_target_pairs={{0,4},{2,6},{4,0},{6,2},{8,12},{10,14},{12,8},{14,10},{16,20},{18,... | collective-permute-start | bytes 221192 | tf_op jit(solution)/shard_map/ppermute | solution.py:162
  45.6 5.0 %collective-permute-start.16 = (bf16[48,768]{1,0:T(8,128)(2,1)S(1)}, bf16[48,768]{1,0:T(8,128)(2,1)S(1)}, u32[]{:S(2)}, u32[]{:S(2)}) collective-permute-start(bf16[48,768]{1,0:T(8,128)(2,1)S(1)} %get-tuple-element.35), channel_id=1, source_target_pairs={{0,8},{2,10},{4,12},{6,14},{8,0},{10,2},{12,4},{14,6},{16,24},{18,... | collective-permute-start | bytes 221192 | tf_op jit(solution)/shard_map/ppermute | solution.py:162
  45.6 6.8 %collective-permute-start.17 = (bf16[48,768]{1,0:T(8,128)(2,1)S(1)}, bf16[48,768]{1,0:T(8,128)(2,1)S(1)}, u32[]{:S(2)}, u32[]{:S(2)}) collective-permute-start(bf16[48,768]{1,0:T(8,128)(2,1)S(1)} %get-tuple-element.36), channel_id=1, source_target_pairs={{0,12},{2,14},{4,8},{6,10},{8,4},{10,6},{12,0},{14,2},{16,28},{18,... | collective-permute-start | bytes 221192 | tf_op jit(solution)/shard_map/ppermute | solution.py:162
where the time goes:
time: 53.4 us; the launch traced here: 53.2 us
  waiting for transfers between devices  30.5 us (57%)
  starting transfers between devices  14.6 us (27%)
  Pallas kernels  5.03 us (9%)
  local copies, waits for them, and re-layouts  2.88 us (5%)
    ppermute x10, waiting for transfers between devices, across(): return lax.ppermute(piece, 'sp', pairs)  30.5 us
    ppermute x10, starting transfers between devices, across(): return lax.ppermute(piece, 'sp', pairs)  13.5 us
    unnamed x6, local copies, waits for them, and re-layouts  2.88 us
    pallas_call x1, Pallas kernels, attend_last(): pl.pallas_call(functools.partial(last_kernel, count=len(pieces), scale=sc...  2.11 us
    pallas_call x1, Pallas kernels, attend_first(): pl.pallas_call(functools.partial(first_kernel, groups=groups, count=len(p...  1.78 us
    ppermute x8, starting transfers between devices, sibling(): return lax.ppermute(piece, 'sp', pairs)  1.15 us
  transfers between devices with their start and end apart: 18, of which 8 were waited for; matrix products, arithmetic and copies ran while one was open for 0% of the time, Pallas kernels for 3%

commit v1 on v0

--- a/solution.py
+++ b/solution.py
@@ -26,12 +26,18 @@
 
 
 def pack_kernel(group_ref, q_ref, k_ref, v_ref, *refs, groups):
-    near, far, wide = refs[:groups], refs[groups : 2 * groups], refs[2 * groups]
+    near, far = refs[:groups], refs[groups : 2 * groups]
+    landed, wide, arrived = refs[2 * groups :]
     tokens, heads, width = q_ref.shape
     per_group = heads // groups
     group = group_ref[0]
+    copies = []
     for part, ref in enumerate((k_ref, v_ref, q_ref)):
-        wide[part] = ref[...].reshape(tokens * heads, width).astype(jnp.float32)
+        copies.append(pltpu.make_async_copy(ref, landed.at[part], arrived.at[part]))
+        copies[part].start()
+    for part in range(3):
+        copies[part].wait()
+        wide[part] = landed[part].reshape(tokens * heads, width).astype(jnp.float32)
         for mask in range(groups):
             first = (group ^ mask) * per_group
             for head in range(per_group):
@@ -47,12 +53,16 @@
     far = pltpu.VMEM((2, heads // groups, tokens, width), queries.dtype)
     outs = pl.pallas_call(
         functools.partial(pack_kernel, groups=groups),
-        in_specs=scalar() + local(3),
+        in_specs=scalar() + [pl.BlockSpec(memory_space=pltpu.MemorySpace.HBM)] * 3,
         out_specs=local(2 * groups),
         out_shape=[near] * groups + [far] * groups,
-        scratch_shapes=[pltpu.VMEM((3, tokens * heads, width), jnp.float32)],
-        compiler_params=PARAMS,
-    )(group, queries, keys, values)
+        scratch_shapes=[
+            pltpu.VMEM((3, tokens, heads, width), queries.dtype),
+            pltpu.VMEM((3, tokens * heads, width), jnp.float32),
+            pltpu.SemaphoreType.DMA((3,)),
+        ],
+        compiler_params=PARAMS,
+    )(group, *(pltpu.with_memory_space_constraint(x, pltpu.MemorySpace.HBM) for x in (queries, keys, values)))
     return outs[:groups], outs[groups:]
 
 
@@ -95,16 +105,43 @@
     )(*map(inside, pieces))
 
 
-def last_kernel(q_ref, largest_ref, total_ref, summed_ref, *refs, count, scale):
-    pieces, outs = refs[:count], refs[count:]
+def merge(refs, pieces, head, scale):
+    q_ref, largest_ref, total_ref, summed_ref = refs
+    largest, total, summed = block(q_ref[head], pieces, head, scale)
+    before = largest_ref[head]
+    top = jnp.maximum(largest, before)
+    now, then = jnp.exp2((largest - top) * scale), jnp.exp2((before - top) * scale)
+    return top, now, then, total * now + total_ref[head] * then, summed, summed_ref[head]
+
+
+def middle_kernel(*refs, count, scale):
+    state, pieces, (largest_out, total_out, summed_out) = refs[:4], refs[4 : 4 + count], refs[4 + count :]
+    for head in range(pieces[0].shape[1]):
+        top, now, then, total, summed, earlier = merge(state, pieces, head, scale)
+        largest_out[head] = top
+        total_out[head] = total
+        summed_out[head] = summed * now + earlier * then
+
+
+def attend_middle(state, pieces, scale):
+    shapes = [pltpu.VMEM(part.shape, part.dtype) for part in state[1:]]
+    outs = pl.pallas_call(
+        functools.partial(middle_kernel, count=len(pieces), scale=scale),
+        in_specs=local(4 + len(pieces)),
+        out_specs=local(3),
+        out_shape=shapes,
+        compiler_params=PARAMS,
+    )(*map(inside, state), *map(inside, pieces))
+    return [state[0]] + list(outs)
+
+
+def last_kernel(*refs, count, scale):
+    state, pieces, outs = refs[:4], refs[4 : 4 + count], refs[4 + count :]
     per_group, tokens, width = pieces[0].shape[1:]
     for head in range(per_group):
-        largest, total, summed = block(q_ref[head], pieces, head, scale)
-        before = largest_ref[head]
-        top = jnp.maximum(largest, before)
-        now, then = jnp.exp2((largest - top) * scale), jnp.exp2((before - top) * scale)
-        inverse = 1.0 / (total * now + total_ref[head] * then)
-        result = summed * (now * inverse) + summed_ref[head] * (then * inverse)
+        _, now, then, total, summed, earlier = merge(state, pieces, head, scale)
+        inverse = 1.0 / total
+        result = summed * (now * inverse) + earlier * (then * inverse)
         result = result.astype(pieces[0].dtype)
         for mask, out in enumerate(outs):
             out[:, head * width : (head + 1) * width] = result[mask * tokens : (mask + 1) * tokens]
@@ -166,7 +203,7 @@
         return lax.ppermute(piece, "sp", pairs)
 
     near, far = pack(group, queries, keys, values, groups)
-    far_in, far_all, near_in, near_all = [], [], [near[0]], []
+    far_in, near_in, near_all = [], [near[0]], []
     for step in range(1, regions):
         for mask in reversed(range(groups)):
             far_in.append(across(far[mask], mask, step))
@@ -174,8 +211,11 @@
         near_in.append(across(near[mask], mask, 0))
     near_all = near_in + [sibling(far[0])] + [sibling(piece) for piece in near_in[1:]]
     state = attend_first(near_all, groups, scale)
-    far_all = far_in + [sibling(piece) for piece in far_in]
-    results = attend_last(state, far_all, groups, scale)
+    half = len(far_in) // 2
+    early = far_in[:half] + [sibling(piece) for piece in far_in[:half]]
+    late = far_in[half:] + [sibling(piece) for piece in far_in[half:]]
+    state = attend_middle(state, early, scale)
+    results = attend_last(state, late, groups, scale)
     returned = [results[0]] + [across(results[mask], mask, 0) for mask in range(1, groups)]
     return unpack(group, returned)
 

time: 53.4 us -> 55.2 us (1.034)
  Pallas kernels: 5.03 us -> 8.72 us
  local copies, waits for them, and re-layouts: 2.88 us -> 0 us
  waiting for transfers between devices: 30.5 us -> 32.3 us
  starting transfers between devices: 14.6 us -> 14 us
    unnamed x6 -> x0, local copies, waits for them, and re-layouts: 2.88 us -> none
    pallas_call x0 -> x1, Pallas kernels: none -> 2.72 us  [attend_middle(): pl.pallas_call(functools.partial(middle_kernel, count=len(pieces), scale=...]
    ppermute x10, waiting for transfers between devices: 30.5 us -> 32.3 us  [across(): return lax.ppermute(piece, 'sp', pairs)]
    pallas_call x1, Pallas kernels: 0.41 us -> 1.4 us  [pack(): pl.pallas_call(functools.partial(pack_kernel, groups=groups), in_specs=sc...]
    ppermute x10, starting transfers between devices: 13.5 us -> 12.9 us  [across(): return lax.ppermute(piece, 'sp', pairs)]
  transfers between devices with their start and end apart: 18 -> 18, of which waited for: 8 -> 8; matrix products, arithmetic and copies ran while one was open for 0% -> 0% of each run, Pallas kernels for 3% -> 8%
where the time goes in v1:
time: 55.2 us; the launch traced here: 55.1 us
  waiting for transfers between devices  32.3 us (59%)
  starting transfers between devices  14 us (25%)
  Pallas kernels  8.72 us (16%)
    ppermute x10, waiting for transfers between devices, across(): return lax.ppermute(piece, 'sp', pairs)  32.3 us
    ppermute x10, starting transfers between devices, across(): return lax.ppermute(piece, 'sp', pairs)  12.9 us
    pallas_call x1, Pallas kernels, attend_middle(): pl.pallas_call(functools.partial(middle_kernel, count=len(pieces), scale=...  2.72 us
    pallas_call x1, Pallas kernels, attend_last(): pl.pallas_call(functools.partial(last_kernel, count=len(pieces), scale=sc...  2.09 us
    pallas_call x1, Pallas kernels, attend_first(): pl.pallas_call(functools.partial(first_kernel, groups=groups, count=len(p...  1.78 us
    pallas_call x1, Pallas kernels, pack(): pl.pallas_call(functools.partial(pack_kernel, groups=groups), in_specs=sc...  1.4 us
    ppermute x8, starting transfers between devices, sibling(): return lax.ppermute(piece, 'sp', pairs)  1.15 us
  transfers between devices with their start and end apart: 18, of which 8 were waited for; matrix products, arithmetic and copies ran while one was open for 0% of the time, Pallas kernels for 8%

profile of v1, /device:TPU:0, one launch (start us, length us, event | category | flops | bytes accessed | tf_op | source)
XLA Modules:
  0.0 55.1 jit_solution(3857863320518333818)
XLA Ops:
  0.0 1.4 %shard_map.37 = (bf16[3,6,48,128]{3,2,1,0:T(8,128)(2,1)S(1)}, bf16[3,6,48,128]{3,2,1,0:T(8,128)(2,1)S(1)}, bf16[3,6,48,128]{3,2,1,0:T(8,128)(2,1)S(1)}, bf16[3,6...) custom-call(s32[1]{0:T(128)} %bitcast.group_ref, ...), custom_call_target="tpu_custom_call" | custom-call | tf_op jit(solution)/shard_map/pallas_call | solution.py:54
  1.4 0.6 %collective-permute-start.3 = (bf16[2,6,48,128]{3,2,1,0:T(8,128)(2,1)S(1)}, bf16[2,6,48,128]{3,2,1,0:T(8,128)(2,1)S(1)}, u32[]{:S(2)}, u32[]{:S(2)}) collective-permute-start(bf16[2,6,48,128]{3,2,1,0:T(8,128)(2,1)S(1)} %get-tuple-element.28), channel_id=1, source_target_pairs={{0,2},{2,0},{4,6},{6,4},{8,10},{10,8},{12,14},{14,12},{16,18},{18,... | collective-permute-start | bytes 442376 | tf_op jit(solution)/shard_map/ppermute | solution.py:203
  2.0 2.6 %collective-permute-start = (bf16[3,6,48,128]{3,2,1,0:T(8,128)(2,1)S(1)}, bf16[3,6,48,128]{3,2,1,0:T(8,128)(2,1)S(1)}, u32[]{:S(2)}, u32[]{:S(2)}) collective-permute-start(bf16[3,6,48,128]{3,2,1,0:T(8,128)(2,1)S(1)} %get-tuple-element.25), channel_id=1, source_target_pairs={{0,4},{2,6},{4,0},{6,2},{8,12},{10,14},{12,8},{14,10},{16,20},{18,... | collective-permute-start | bytes 663560 | tf_op jit(solution)/shard_map/ppermute | solution.py:199
  4.5 1.6 %collective-permute-start.1 = (bf16[3,6,48,128]{3,2,1,0:T(8,128)(2,1)S(1)}, bf16[3,6,48,128]{3,2,1,0:T(8,128)(2,1)S(1)}, u32[]{:S(2)}, u32[]{:S(2)}) collective-permute-start(bf16[3,6,48,128]{3,2,1,0:T(8,128)(2,1)S(1)} %get-tuple-element.26), channel_id=1, source_target_pairs={{0,8},{2,10},{4,12},{6,14},{8,0},{10,2},{12,4},{14,6},{16,24},{18,... | collective-permute-start | bytes 663560 | tf_op jit(solution)/shard_map/ppermute | solution.py:199
  6.1 4.0 %collective-permute-start.8 = (bf16[2,6,48,128]{3,2,1,0:T(8,128)(2,1)S(1)}, bf16[2,6,48,128]{3,2,1,0:T(8,128)(2,1)S(1)}, u32[]{:S(2)}, u32[]{:S(2)}) collective-permute-start(bf16[2,6,48,128]{3,2,1,0:T(8,128)(2,1)S(1)} %get-tuple-element.34), channel_id=1, source_target_pairs={{0,24},{2,26},{4,28},{6,30},{8,16},{10,18},{12,20},{14,22},{16,8},... | collective-permute-start | bytes 442376 | tf_op jit(solution)/shard_map/ppermute | solution.py:199
  10.1 1.2 %collective-permute-start.7 = (bf16[2,6,48,128]{3,2,1,0:T(8,128)(2,1)S(1)}, bf16[2,6,48,128]{3,2,1,0:T(8,128)(2,1)S(1)}, u32[]{:S(2)}, u32[]{:S(2)}) collective-permute-start(bf16[2,6,48,128]{3,2,1,0:T(8,128)(2,1)S(1)} %get-tuple-element.33), channel_id=1, source_target_pairs={{0,28},{2,30},{4,24},{6,26},{8,20},{10,22},{12,16},{14,18},{16,12}... | collective-permute-start | bytes 442376 | tf_op jit(solution)/shard_map/ppermute | solution.py:199
  11.3 0.0 collective-permute-done.refs_1_
  11.3 0.0 collective-permute-start.4
  11.3 1.5 %collective-permute-done.1.refs_2_ = bf16[3,6,48,128]{3,2,1,0:T(8,128)(2,1)S(1)} collective-permute-done((bf16[3,6,48,128]{3,2,1,0:T(8,128)(2,1)S(1)}, bf16[3,6,48,128]{3,2,1,0:T(8,128)(2,1)S(1)}, u32[]{:S(2)}, u32[]{:S(2)}) %collective-permute-start.1) | collective-permute-done | bytes 221216 | tf_op jit(solution)/shard_map/ppermute | solution.py:199
  12.8 0.0 collective-permute-start.5
  12.8 11.9 %collective-permute-done.8.refs_5_ = bf16[2,6,48,128]{3,2,1,0:T(8,128)(2,1)S(1)} collective-permute-done((bf16[2,6,48,128]{3,2,1,0:T(8,128)(2,1)S(1)}, bf16[2,6,48,128]{3,2,1,0:T(8,128)(2,1)S(1)}, u32[]{:S(2)}, u32[]{:S(2)}) %collective-permute-start.8) | collective-permute-done | bytes 147488 | tf_op jit(solution)/shard_map/ppermute | solution.py:199
  24.7 2.9 %collective-permute-done.7.refs_4_ = bf16[2,6,48,128]{3,2,1,0:T(8,128)(2,1)S(1)} collective-permute-done((bf16[2,6,48,128]{3,2,1,0:T(8,128)(2,1)S(1)}, bf16[2,6,48,128]{3,2,1,0:T(8,128)(2,1)S(1)}, u32[]{:S(2)}, u32[]{:S(2)}) %collective-permute-start.7) | collective-permute-done | bytes 147488 | tf_op jit(solution)/shard_map/ppermute | solution.py:199
  27.6 0.0 collective-permute-start.12
  27.6 0.0 collective-permute-done.2.refs_3_
  27.6 0.0 collective-permute-start.6
  27.6 8.7 %collective-permute-done.11.refs_4_ = bf16[2,6,48,128]{3,2,1,0:T(8,128)(2,1)S(1)} collective-permute-done((bf16[2,6,48,128]{3,2,1,0:T(8,128)(2,1)S(1)}, bf16[2,6,48,128]{3,2,1,0:T(8,128)(2,1)S(1)}, u32[]{:S(2)}, u32[]{:S(2)}) %collective-permute-start.11) | collective-permute-done | bytes 147488 | tf_op jit(solution)/shard_map/ppermute | solution.py:199
  36.4 0.0 collective-permute-start.10
  36.4 3.3 %collective-permute-done.12.refs_5_ = bf16[2,6,48,128]{3,2,1,0:T(8,128)(2,1)S(1)} collective-permute-done((bf16[2,6,48,128]{3,2,1,0:T(8,128)(2,1)S(1)}, bf16[2,6,48,128]{3,2,1,0:T(8,128)(2,1)S(1)}, u32[]{:S(2)}, u32[]{:S(2)}) %collective-permute-start.12) | collective-permute-done | bytes 147488 | tf_op jit(solution)/shard_map/ppermute | solution.py:199
  39.7 0.0 collective-permute-start.9
  39.7 0.0 collective-permute-done.4.refs_5_
  39.7 0.5 collective-permute-start.13
  40.2 0.0 collective-permute-done.5.refs_6_
  40.2 0.1 collective-permute-start.14
  40.3 1.8 %shard_map.38 = (bf16[6,192,128]{2,1,0:T(8,128)(2,1)S(1)}, f32[6,192,1]{2,1,0:T(8,128)S(1)}, f32[6,192,1]{2,1,0:T(8,128)S(1)}, f32[6,192,128]{2,1,0:T(8,128)S(1)}) custom-call(bf16[3,6,48,128]{3,2,1,0:T(8,128)(2,1)S(1)} %get-tuple-element.24.refs_0_, bf16[3,6,48,128]{3,2,1,0:T(8,128)(2,1)S(1)} %collective-permute-done.refs_1_, ...), custom_call_target="tpu_custom_call" | custom-call | tf_op jit(solution)/shard_map/pallas_call | solution.py:94
  42.1 2.7 %shard_map.39 = (f32[6,192,1]{2,1,0:T(8,128)S(1)}, f32[6,192,1]{2,1,0:T(8,128)S(1)}, f32[6,192,128]{2,1,0:T(8,128)S(1)}) custom-call(bf16[6,192,128]{2,1,0:T(8,128)(2,1)S(1)} %get-tuple-element.29.refs_0_, f32[6,192,1]{2,1,0:T(8,128)S(1)} %get-tuple-element.30.refs_1_, f32[6,192,1]{2,1,0:T(8,128)S(1)} %get-tuple-element.31.refs_2_, ...), custom_call_target="tpu_custom_call" | custom-call | tf_op jit(solution)/shard_map/pallas_call | solution.py:128
  44.8 2.1 %shard_map.40 = (bf16[48,768]{1,0:T(8,128)(2,1)S(1)}, bf16[48,768]{1,0:T(8,128)(2,1)S(1)}, bf16[48,768]{1,0:T(8,128)(2,1)S(1)}, bf16[48,768]{1,0:T(8,128)(2,1)S(1)}) custom-call(bf16[6,192,128]{2,1,0:T(8,128)(2,1)S(1)} %get-tuple-element.29.refs_0_, f32[6,192,1]{2,1,0:T(8,128)S(1)} %get-tuple-element.35.refs_1_, f32[6,192,1]{2,1,0:T(8,128)S(1)} %get-tuple-element.36.refs_2_, ...), custom_call_target="tpu_custom_call" | custom-call | tf_op jit(solution)/shard_map/pallas_call | solution.py:153
  46.9 0.4 collective-permute-start.15
  47.3 3.2 %collective-permute-start.17 = (bf16[48,768]{1,0:T(8,128)(2,1)S(1)}, bf16[48,768]{1,0:T(8,128)(2,1)S(1)}, u32[]{:S(2)}, u32[]{:S(2)}) collective-permute-start(bf16[48,768]{1,0:T(8,128)(2,1)S(1)} %get-tuple-element.42), channel_id=1, source_target_pairs={{0,12},{2,14},{4,8},{6,10},{8,4},{10,6},{12,0},{14,2},{16,28},{18,... | collective-permute-start | bytes 221192 | tf_op jit(solution)/shard_map/ppermute | solution.py:199
  50.5 1.1 %collective-permute-done.15.refs_1_ = bf16[48,768]{1,0:T(8,128)(2,1)S(1)} collective-permute-done((bf16[48,768]{1,0:T(8,128)(2,1)S(1)}, bf16[48,768]{1,0:T(8,128)(2,1)S(1)}, u32[]{:S(2)}, u32[]{:S(2)}) %collective-permute-start.15) | collective-permute-done | bytes 73760 | tf_op jit(solution)/shard_map/ppermute | solution.py:199
  51.6 0.6 collective-permute-done.16.refs_2_
  52.1 2.2 %collective-permute-done.17.refs_3_ = bf16[48,768]{1,0:T(8,128)(2,1)S(1)} collective-permute-done((bf16[48,768]{1,0:T(8,128)(2,1)S(1)}, bf16[48,768]{1,0:T(8,128)(2,1)S(1)}, u32[]{:S(2)}, u32[]{:S(2)}) %collective-permute-start.17) | collective-permute-done | bytes 73760 | tf_op jit(solution)/shard_map/ppermute | solution.py:199
  54.3 0.7 %shard_map.41 = bf16[48,3072]{1,0:T(8,128)(2,1)} custom-call(s32[1]{0:T(128)} %bitcast.group_ref, bf16[48,768]{1,0:T(8,128)(2,1)S(1)} %get-tuple-element.39.refs_0_, bf16[48,768]{1,0:T(8,128)(2,1)S(1)} %collective-permute-done.15.refs_1_, bf16[48,768]{1,0:T(8,128)(2,1)S(1)} %collective-permute-done.16.refs_2_, ...), custom_call_target="tpu_custom_call" | custom-call | tf_op jit(solution)/shard_map/pallas_call | solution.py:173
  (9 shorter events, 0.0 us)
Async XLA Ops:
  1.4 8.7 %collective-permute-start.3 = (bf16[2,6,48,128]{3,2,1,0:T(8,128)(2,1)S(1)}, bf16[2,6,48,128]{3,2,1,0:T(8,128)(2,1)S(1)}, u32[]{:S(2)}, u32[]{:S(2)}) collective-permute-start(bf16[2,6,48,128]{3,2,1,0:T(8,128)(2,1)S(1)} %get-tuple-element.28), channel_id=1, source_target_pairs={{0,2},{2,0},{4,6},{6,4},{8,10},{10,8},{12,14},{14,12},{16,18},{18,... | collective-permute-start | bytes 442376 | tf_op jit(solution)/shard_map/ppermute | solution.py:203
  2.0 9.3 %collective-permute-start = (bf16[3,6,48,128]{3,2,1,0:T(8,128)(2,1)S(1)}, bf16[3,6,48,128]{3,2,1,0:T(8,128)(2,1)S(1)}, u32[]{:S(2)}, u32[]{:S(2)}) collective-permute-start(bf16[3,6,48,128]{3,2,1,0:T(8,128)(2,1)S(1)} %get-tuple-element.25), channel_id=1, source_target_pairs={{0,4},{2,6},{4,0},{6,2},{8,12},{10,14},{12,8},{14,10},{16,20},{18,... | collective-permute-start | bytes 663560 | tf_op jit(solution)/shard_map/ppermute | solution.py:199
  4.5 8.3 %collective-permute-start.1 = (bf16[3,6,48,128]{3,2,1,0:T(8,128)(2,1)S(1)}, bf16[3,6,48,128]{3,2,1,0:T(8,128)(2,1)S(1)}, u32[]{:S(2)}, u32[]{:S(2)}) collective-permute-start(bf16[3,6,48,128]{3,2,1,0:T(8,128)(2,1)S(1)} %get-tuple-element.26), channel_id=1, source_target_pairs={{0,8},{2,10},{4,12},{6,14},{8,0},{10,2},{12,4},{14,6},{16,24},{18,... | collective-permute-start | bytes 663560 | tf_op jit(solution)/shard_map/ppermute | solution.py:199
  6.1 21.5 %collective-permute-start.2 = (bf16[3,6,48,128]{3,2,1,0:T(8,128)(2,1)S(1)}, bf16[3,6,48,128]{3,2,1,0:T(8,128)(2,1)S(1)}, u32[]{:S(2)}, u32[]{:S(2)}) collective-permute-start(bf16[3,6,48,128]{3,2,1,0:T(8,128)(2,1)S(1)} %get-tuple-element.27), channel_id=1, source_target_pairs={{0,12},{2,14},{4,8},{6,10},{8,4},{10,6},{12,0},{14,2},{16,28},{18,... | collective-permute-start | bytes 663560 | tf_op jit(solution)/shard_map/ppermute | solution.py:199
  6.1 18.6 %collective-permute-start.8 = (bf16[2,6,48,128]{3,2,1,0:T(8,128)(2,1)S(1)}, bf16[2,6,48,128]{3,2,1,0:T(8,128)(2,1)S(1)}, u32[]{:S(2)}, u32[]{:S(2)}) collective-permute-start(bf16[2,6,48,128]{3,2,1,0:T(8,128)(2,1)S(1)} %get-tuple-element.34), channel_id=1, source_target_pairs={{0,24},{2,26},{4,28},{6,30},{8,16},{10,18},{12,20},{14,22},{16,8},... | collective-permute-start | bytes 442376 | tf_op jit(solution)/shard_map/ppermute | solution.py:199
  10.1 17.5 %collective-permute-start.7 = (bf16[2,6,48,128]{3,2,1,0:T(8,128)(2,1)S(1)}, bf16[2,6,48,128]{3,2,1,0:T(8,128)(2,1)S(1)}, u32[]{:S(2)}, u32[]{:S(2)}) collective-permute-start(bf16[2,6,48,128]{3,2,1,0:T(8,128)(2,1)S(1)} %get-tuple-element.33), channel_id=1, source_target_pairs={{0,28},{2,30},{4,24},{6,26},{8,20},{10,22},{12,16},{14,18},{16,12}... | collective-permute-start | bytes 442376 | tf_op jit(solution)/shard_map/ppermute | solution.py:199
  11.3 28.4 %collective-permute-start.4 = (bf16[3,6,48,128]{3,2,1,0:T(8,128)(2,1)S(1)}, bf16[3,6,48,128]{3,2,1,0:T(8,128)(2,1)S(1)}, u32[]{:S(2)}, u32[]{:S(2)}) collective-permute-start(bf16[3,6,48,128]{3,2,1,0:T(8,128)(2,1)S(1)} %collective-permute-done.refs_1_), channel_id=1, source_target_pairs={{0,2},{2,0},{4,6},{6,4},{8,10},{10,8},{12,14},{14,12},{16,18},{18,... | collective-permute-start | bytes 663560 | tf_op jit(solution)/shard_map/ppermute | solution.py:203
  12.8 27.4 %collective-permute-start.5 = (bf16[3,6,48,128]{3,2,1,0:T(8,128)(2,1)S(1)}, bf16[3,6,48,128]{3,2,1,0:T(8,128)(2,1)S(1)}, u32[]{:S(2)}, u32[]{:S(2)}) collective-permute-start(bf16[3,6,48,128]{3,2,1,0:T(8,128)(2,1)S(1)} %collective-permute-done.1.refs_2_), channel_id=1, source_target_pairs={{0,2},{2,0},{4,6},{6,4},{8,10},{10,8},{12,14},{14,12},{16,18},{18,... | collective-permute-start | bytes 663560 | tf_op jit(solution)/shard_map/ppermute | solution.py:203
  24.7 11.7 %collective-permute-start.11 = (bf16[2,6,48,128]{3,2,1,0:T(8,128)(2,1)S(1)}, bf16[2,6,48,128]{3,2,1,0:T(8,128)(2,1)S(1)}, u32[]{:S(2)}, u32[]{:S(2)}) collective-permute-start(bf16[2,6,48,128]{3,2,1,0:T(8,128)(2,1)S(1)} %get-tuple-element.38), channel_id=1, source_target_pairs={{0,20},{2,22},{4,16},{6,18},{8,28},{10,30},{12,24},{14,26},{16,4},... | collective-permute-start | bytes 442376 | tf_op jit(solution)/shard_map/ppermute | solution.py:199
  27.6 12.1 %collective-permute-start.12 = (bf16[2,6,48,128]{3,2,1,0:T(8,128)(2,1)S(1)}, bf16[2,6,48,128]{3,2,1,0:T(8,128)(2,1)S(1)}, u32[]{:S(2)}, u32[]{:S(2)}) collective-permute-start(bf16[2,6,48,128]{3,2,1,0:T(8,128)(2,1)S(1)} %get-tuple-element.28), channel_id=1, source_target_pairs={{0,16},{2,18},{4,20},{6,22},{8,24},{10,26},{12,28},{14,30},{16,0},... | collective-permute-start | bytes 442376 | tf_op jit(solution)/shard_map/ppermute | solution.py:199
  27.6 12.7 %collective-permute-start.6 = (bf16[3,6,48,128]{3,2,1,0:T(8,128)(2,1)S(1)}, bf16[3,6,48,128]{3,2,1,0:T(8,128)(2,1)S(1)}, u32[]{:S(2)}, u32[]{:S(2)}) collective-permute-start(bf16[3,6,48,128]{3,2,1,0:T(8,128)(2,1)S(1)} %collective-permute-done.2.refs_3_), channel_id=1, source_target_pairs={{0,2},{2,0},{4,6},{6,4},{8,10},{10,8},{12,14},{14,12},{16,18},{18,... | collective-permute-start | bytes 663560 | tf_op jit(solution)/shard_map/ppermute | solution.py:203
  36.4 5.7 %collective-permute-start.10 = (bf16[2,6,48,128]{3,2,1,0:T(8,128)(2,1)S(1)}, bf16[2,6,48,128]{3,2,1,0:T(8,128)(2,1)S(1)}, u32[]{:S(2)}, u32[]{:S(2)}) collective-permute-start(bf16[2,6,48,128]{3,2,1,0:T(8,128)(2,1)S(1)} %collective-permute-done.8.refs_5_), channel_id=1, source_target_pairs={{0,2},{2,0},{4,6},{6,4},{8,10},{10,8},{12,14},{14,12},{16,18},{18,... | collective-permute-start | bytes 442376 | tf_op jit(solution)/shard_map/ppermute | solution.py:203
  39.7 2.4 %collective-permute-start.9 = (bf16[2,6,48,128]{3,2,1,0:T(8,128)(2,1)S(1)}, bf16[2,6,48,128]{3,2,1,0:T(8,128)(2,1)S(1)}, u32[]{:S(2)}, u32[]{:S(2)}) collective-permute-start(bf16[2,6,48,128]{3,2,1,0:T(8,128)(2,1)S(1)} %collective-permute-done.7.refs_4_), channel_id=1, source_target_pairs={{0,2},{2,0},{4,6},{6,4},{8,10},{10,8},{12,14},{14,12},{16,18},{18,... | collective-permute-start | bytes 442376 | tf_op jit(solution)/shard_map/ppermute | solution.py:203
  39.7 5.1 %collective-permute-start.13 = (bf16[2,6,48,128]{3,2,1,0:T(8,128)(2,1)S(1)}, bf16[2,6,48,128]{3,2,1,0:T(8,128)(2,1)S(1)}, u32[]{:S(2)}, u32[]{:S(2)}) collective-permute-start(bf16[2,6,48,128]{3,2,1,0:T(8,128)(2,1)S(1)} %collective-permute-done.11.refs_4_), channel_id=1, source_target_pairs={{0,2},{2,0},{4,6},{6,4},{8,10},{10,8},{12,14},{14,12},{16,18},{18,... | collective-permute-start | bytes 442376 | tf_op jit(solution)/shard_map/ppermute | solution.py:203
  40.2 4.6 %collective-permute-start.14 = (bf16[2,6,48,128]{3,2,1,0:T(8,128)(2,1)S(1)}, bf16[2,6,48,128]{3,2,1,0:T(8,128)(2,1)S(1)}, u32[]{:S(2)}, u32[]{:S(2)}) collective-permute-start(bf16[2,6,48,128]{3,2,1,0:T(8,128)(2,1)S(1)} %collective-permute-done.12.refs_5_), channel_id=1, source_target_pairs={{0,2},{2,0},{4,6},{6,4},{8,10},{10,8},{12,14},{14,12},{16,18},{18,... | collective-permute-start | bytes 442376 | tf_op jit(solution)/shard_map/ppermute | solution.py:203
  46.9 4.7 %collective-permute-start.15 = (bf16[48,768]{1,0:T(8,128)(2,1)S(1)}, bf16[48,768]{1,0:T(8,128)(2,1)S(1)}, u32[]{:S(2)}, u32[]{:S(2)}) collective-permute-start(bf16[48,768]{1,0:T(8,128)(2,1)S(1)} %get-tuple-element.40), channel_id=1, source_target_pairs={{0,4},{2,6},{4,0},{6,2},{8,12},{10,14},{12,8},{14,10},{16,20},{18,... | collective-permute-start | bytes 221192 | tf_op jit(solution)/shard_map/ppermute | solution.py:199
  47.3 4.8 %collective-permute-start.16 = (bf16[48,768]{1,0:T(8,128)(2,1)S(1)}, bf16[48,768]{1,0:T(8,128)(2,1)S(1)}, u32[]{:S(2)}, u32[]{:S(2)}) collective-permute-start(bf16[48,768]{1,0:T(8,128)(2,1)S(1)} %get-tuple-element.41), channel_id=1, source_target_pairs={{0,8},{2,10},{4,12},{6,14},{8,0},{10,2},{12,4},{14,6},{16,24},{18,... | collective-permute-start | bytes 221192 | tf_op jit(solution)/shard_map/ppermute | solution.py:199
  47.3 7.1 %collective-permute-start.17 = (bf16[48,768]{1,0:T(8,128)(2,1)S(1)}, bf16[48,768]{1,0:T(8,128)(2,1)S(1)}, u32[]{:S(2)}, u32[]{:S(2)}) collective-permute-start(bf16[48,768]{1,0:T(8,128)(2,1)S(1)} %get-tuple-element.42), channel_id=1, source_target_pairs={{0,12},{2,14},{4,8},{6,10},{8,4},{10,6},{12,0},{14,2},{16,28},{18,... | collective-permute-start | bytes 221192 | tf_op jit(solution)/shard_map/ppermute | solution.py:199

commit v2 on v1

--- a/solution.py
+++ b/solution.py
@@ -114,27 +114,6 @@
     return top, now, then, total * now + total_ref[head] * then, summed, summed_ref[head]
 
 
-def middle_kernel(*refs, count, scale):
-    state, pieces, (largest_out, total_out, summed_out) = refs[:4], refs[4 : 4 + count], refs[4 + count :]
-    for head in range(pieces[0].shape[1]):
-        top, now, then, total, summed, earlier = merge(state, pieces, head, scale)
-        largest_out[head] = top
-        total_out[head] = total
-        summed_out[head] = summed * now + earlier * then
-
-
-def attend_middle(state, pieces, scale):
-    shapes = [pltpu.VMEM(part.shape, part.dtype) for part in state[1:]]
-    outs = pl.pallas_call(
-        functools.partial(middle_kernel, count=len(pieces), scale=scale),
-        in_specs=local(4 + len(pieces)),
-        out_specs=local(3),
-        out_shape=shapes,
-        compiler_params=PARAMS,
-    )(*map(inside, state), *map(inside, pieces))
-    return [state[0]] + list(outs)
-
-
 def last_kernel(*refs, count, scale):
     state, pieces, outs = refs[:4], refs[4 : 4 + count], refs[4 + count :]
     per_group, tokens, width = pieces[0].shape[1:]
@@ -203,7 +182,7 @@
         return lax.ppermute(piece, "sp", pairs)
 
     near, far = pack(group, queries, keys, values, groups)
-    far_in, near_in, near_all = [], [near[0]], []
+    far_in, far_all, near_in, near_all = [], [], [near[0]], []
     for step in range(1, regions):
         for mask in reversed(range(groups)):
             far_in.append(across(far[mask], mask, step))
@@ -211,11 +190,8 @@
         near_in.append(across(near[mask], mask, 0))
     near_all = near_in + [sibling(far[0])] + [sibling(piece) for piece in near_in[1:]]
     state = attend_first(near_all, groups, scale)
-    half = len(far_in) // 2
-    early = far_in[:half] + [sibling(piece) for piece in far_in[:half]]
-    late = far_in[half:] + [sibling(piece) for piece in far_in[half:]]
-    state = attend_middle(state, early, scale)
-    results = attend_last(state, late, groups, scale)
+    far_all = far_in + [sibling(piece) for piece in far_in]
+    results = attend_last(state, far_all, groups, scale)
     returned = [results[0]] + [across(results[mask], mask, 0) for mask in range(1, groups)]
     return unpack(group, returned)
 

time: 55.2 us -> 51.4 us (0.931)
  Pallas kernels: 8.72 us -> 6 us
  waiting for transfers between devices: 32.3 us -> 30.5 us
  starting transfers between devices: 14 us -> 14.6 us
    pallas_call x1 -> x0, Pallas kernels: 2.72 us -> none  [attend_middle(): pl.pallas_call(functools.partial(middle_kernel, count=len(pieces), scale=...]
    ppermute x10, waiting for transfers between devices: 32.3 us -> 30.5 us  [across(): return lax.ppermute(piece, 'sp', pairs)]
    ppermute x10, starting transfers between devices: 12.9 us -> 13.5 us  [across(): return lax.ppermute(piece, 'sp', pairs)]
  transfers between devices with their start and end apart: 18 -> 18, of which waited for: 8 -> 8; matrix products, arithmetic and copies ran while one was open for 0% -> 0% of each run, Pallas kernels for 8% -> 3%
where the time goes in v2:
time: 51.4 us; the launch traced here: 51.2 us
  waiting for transfers between devices  30.5 us (59%)
  starting transfers between devices  14.6 us (28%)
  Pallas kernels  6 us (12%)
    ppermute x10, waiting for transfers between devices, across(): return lax.ppermute(piece, 'sp', pairs)  30.5 us
    ppermute x10, starting transfers between devices, across(): return lax.ppermute(piece, 'sp', pairs)  13.5 us
    pallas_call x1, Pallas kernels, attend_last(): pl.pallas_call(functools.partial(last_kernel, count=len(pieces), scale=sc...  2.09 us
    pallas_call x1, Pallas kernels, attend_first(): pl.pallas_call(functools.partial(first_kernel, groups=groups, count=len(p...  1.78 us
    pallas_call x1, Pallas kernels, pack(): pl.pallas_call(functools.partial(pack_kernel, groups=groups), in_specs=sc...  1.4 us
    ppermute x8, starting transfers between devices, sibling(): return lax.ppermute(piece, 'sp', pairs)  1.15 us
  transfers between devices with their start and end apart: 18, of which 8 were waited for; matrix products, arithmetic and copies ran while one was open for 0% of the time, Pallas kernels for 3%

profile of v2, /device:TPU:0, one launch (start us, length us, event | category | flops | bytes accessed | tf_op | source)
XLA Modules:
  0.0 51.2 jit_solution(7998671194010635955)
XLA Ops:
  0.0 1.4 %shard_map.37 = (bf16[3,6,48,128]{3,2,1,0:T(8,128)(2,1)S(1)}, bf16[3,6,48,128]{3,2,1,0:T(8,128)(2,1)S(1)}, bf16[3,6,48,128]{3,2,1,0:T(8,128)(2,1)S(1)}, bf16[3,6...) custom-call(s32[1]{0:T(128)} %bitcast.group_ref, ...), custom_call_target="tpu_custom_call" | custom-call | tf_op jit(solution)/shard_map/pallas_call | solution.py:54
  1.4 0.6 %collective-permute-start.3 = (bf16[2,6,48,128]{3,2,1,0:T(8,128)(2,1)S(1)}, bf16[2,6,48,128]{3,2,1,0:T(8,128)(2,1)S(1)}, u32[]{:S(2)}, u32[]{:S(2)}) collective-permute-start(bf16[2,6,48,128]{3,2,1,0:T(8,128)(2,1)S(1)} %get-tuple-element.25), channel_id=1, source_target_pairs={{0,2},{2,0},{4,6},{6,4},{8,10},{10,8},{12,14},{14,12},{16,18},{18,... | collective-permute-start | bytes 442376 | tf_op jit(solution)/shard_map/ppermute | solution.py:182
  2.0 2.6 %collective-permute-start = (bf16[3,6,48,128]{3,2,1,0:T(8,128)(2,1)S(1)}, bf16[3,6,48,128]{3,2,1,0:T(8,128)(2,1)S(1)}, u32[]{:S(2)}, u32[]{:S(2)}) collective-permute-start(bf16[3,6,48,128]{3,2,1,0:T(8,128)(2,1)S(1)} %get-tuple-element.22), channel_id=1, source_target_pairs={{0,4},{2,6},{4,0},{6,2},{8,12},{10,14},{12,8},{14,10},{16,20},{18,... | collective-permute-start | bytes 663560 | tf_op jit(solution)/shard_map/ppermute | solution.py:178
  4.5 1.6 %collective-permute-start.1 = (bf16[3,6,48,128]{3,2,1,0:T(8,128)(2,1)S(1)}, bf16[3,6,48,128]{3,2,1,0:T(8,128)(2,1)S(1)}, u32[]{:S(2)}, u32[]{:S(2)}) collective-permute-start(bf16[3,6,48,128]{3,2,1,0:T(8,128)(2,1)S(1)} %get-tuple-element.23), channel_id=1, source_target_pairs={{0,8},{2,10},{4,12},{6,14},{8,0},{10,2},{12,4},{14,6},{16,24},{18,... | collective-permute-start | bytes 663560 | tf_op jit(solution)/shard_map/ppermute | solution.py:178
  6.1 4.9 %collective-permute-start.7 = (bf16[2,6,48,128]{3,2,1,0:T(8,128)(2,1)S(1)}, bf16[2,6,48,128]{3,2,1,0:T(8,128)(2,1)S(1)}, u32[]{:S(2)}, u32[]{:S(2)}) collective-permute-start(bf16[2,6,48,128]{3,2,1,0:T(8,128)(2,1)S(1)} %get-tuple-element.30), channel_id=1, source_target_pairs={{0,28},{2,30},{4,24},{6,26},{8,20},{10,22},{12,16},{14,18},{16,12}... | collective-permute-start | bytes 442376 | tf_op jit(solution)/shard_map/ppermute | solution.py:178
  11.0 0.0 collective-permute-done.3.refs_4_
  11.1 0.2 collective-permute-start.8
  11.3 0.0 collective-permute-done.refs_1_
  11.3 0.0 collective-permute-start.4
  11.3 1.5 %collective-permute-done.1.refs_2_ = bf16[3,6,48,128]{3,2,1,0:T(8,128)(2,1)S(1)} collective-permute-done((bf16[3,6,48,128]{3,2,1,0:T(8,128)(2,1)S(1)}, bf16[3,6,48,128]{3,2,1,0:T(8,128)(2,1)S(1)}, u32[]{:S(2)}, u32[]{:S(2)}) %collective-permute-start.1) | collective-permute-done | bytes 221216 | tf_op jit(solution)/shard_map/ppermute | solution.py:178
  12.8 0.0 collective-permute-start.5
  12.8 10.7 %collective-permute-done.7.refs_4_ = bf16[2,6,48,128]{3,2,1,0:T(8,128)(2,1)S(1)} collective-permute-done((bf16[2,6,48,128]{3,2,1,0:T(8,128)(2,1)S(1)}, bf16[2,6,48,128]{3,2,1,0:T(8,128)(2,1)S(1)}, u32[]{:S(2)}, u32[]{:S(2)}) %collective-permute-start.7) | collective-permute-done | bytes 147488 | tf_op jit(solution)/shard_map/ppermute | solution.py:178
  23.6 3.2 %collective-permute-done.8.refs_5_ = bf16[2,6,48,128]{3,2,1,0:T(8,128)(2,1)S(1)} collective-permute-done((bf16[2,6,48,128]{3,2,1,0:T(8,128)(2,1)S(1)}, bf16[2,6,48,128]{3,2,1,0:T(8,128)(2,1)S(1)}, u32[]{:S(2)}, u32[]{:S(2)}) %collective-permute-start.8) | collective-permute-done | bytes 147488 | tf_op jit(solution)/shard_map/ppermute | solution.py:178
  26.8 0.6 %collective-permute-start.10 = (bf16[2,6,48,128]{3,2,1,0:T(8,128)(2,1)S(1)}, bf16[2,6,48,128]{3,2,1,0:T(8,128)(2,1)S(1)}, u32[]{:S(2)}, u32[]{:S(2)}) collective-permute-start(bf16[2,6,48,128]{3,2,1,0:T(8,128)(2,1)S(1)} %get-tuple-element.25), channel_id=1, source_target_pairs={{0,16},{2,18},{4,20},{6,22},{8,24},{10,26},{12,28},{14,30},{16,0},... | collective-permute-start | bytes 442376 | tf_op jit(solution)/shard_map/ppermute | solution.py:178
  27.4 0.0 collective-permute-done.2.refs_3_
  27.4 0.0 collective-permute-start.6
  27.4 8.1 %collective-permute-done.9.refs_6_ = bf16[2,6,48,128]{3,2,1,0:T(8,128)(2,1)S(1)} collective-permute-done((bf16[2,6,48,128]{3,2,1,0:T(8,128)(2,1)S(1)}, bf16[2,6,48,128]{3,2,1,0:T(8,128)(2,1)S(1)}, u32[]{:S(2)}, u32[]{:S(2)}) %collective-permute-start.9) | collective-permute-done | bytes 147488 | tf_op jit(solution)/shard_map/ppermute | solution.py:178
  35.5 0.0 collective-permute-start.11
  35.5 3.1 %collective-permute-done.10.refs_7_ = bf16[2,6,48,128]{3,2,1,0:T(8,128)(2,1)S(1)} collective-permute-done((bf16[2,6,48,128]{3,2,1,0:T(8,128)(2,1)S(1)}, bf16[2,6,48,128]{3,2,1,0:T(8,128)(2,1)S(1)}, u32[]{:S(2)}, u32[]{:S(2)}) %collective-permute-start.10) | collective-permute-done | bytes 147488 | tf_op jit(solution)/shard_map/ppermute | solution.py:178
  38.6 0.0 collective-permute-start.12
  38.6 0.0 collective-permute-done.4.refs_5_
  38.6 0.5 collective-permute-start.13
  39.1 0.1 collective-permute-start.14
  39.2 1.8 %shard_map.38 = (bf16[6,192,128]{2,1,0:T(8,128)(2,1)S(1)}, f32[6,192,1]{2,1,0:T(8,128)S(1)}, f32[6,192,1]{2,1,0:T(8,128)S(1)}, f32[6,192,128]{2,1,0:T(8,128)S(1)}) custom-call(bf16[3,6,48,128]{3,2,1,0:T(8,128)(2,1)S(1)} %get-tuple-element.21.refs_0_, bf16[3,6,48,128]{3,2,1,0:T(8,128)(2,1)S(1)} %collective-permute-done.refs_1_, ...), custom_call_target="tpu_custom_call" | custom-call | tf_op jit(solution)/shard_map/pallas_call | solution.py:94
  41.0 0.0 collective-permute-done.13.refs_10_
  41.0 2.1 %shard_map.39 = (bf16[48,768]{1,0:T(8,128)(2,1)S(1)}, bf16[48,768]{1,0:T(8,128)(2,1)S(1)}, bf16[48,768]{1,0:T(8,128)(2,1)S(1)}, bf16[48,768]{1,0:T(8,128)(2,1)S(1)}) custom-call(bf16[6,192,128]{2,1,0:T(8,128)(2,1)S(1)} %get-tuple-element.26.refs_0_, f32[6,192,1]{2,1,0:T(8,128)S(1)} %get-tuple-element.27.refs_1_, f32[6,192,1]{2,1,0:T(8,128)S(1)} %get-tuple-element.28.refs_2_, ...), custom_call_target="tpu_custom_call" | custom-call | tf_op jit(solution)/shard_map/pallas_call | solution.py:132
  43.1 0.6 %collective-permute-start.15 = (bf16[48,768]{1,0:T(8,128)(2,1)S(1)}, bf16[48,768]{1,0:T(8,128)(2,1)S(1)}, u32[]{:S(2)}, u32[]{:S(2)}) collective-permute-start(bf16[48,768]{1,0:T(8,128)(2,1)S(1)} %get-tuple-element.34), channel_id=1, source_target_pairs={{0,4},{2,6},{4,0},{6,2},{8,12},{10,14},{12,8},{14,10},{16,20},{18,... | collective-permute-start | bytes 221192 | tf_op jit(solution)/shard_map/ppermute | solution.py:178
  43.7 3.0 %collective-permute-start.17 = (bf16[48,768]{1,0:T(8,128)(2,1)S(1)}, bf16[48,768]{1,0:T(8,128)(2,1)S(1)}, u32[]{:S(2)}, u32[]{:S(2)}) collective-permute-start(bf16[48,768]{1,0:T(8,128)(2,1)S(1)} %get-tuple-element.36), channel_id=1, source_target_pairs={{0,12},{2,14},{4,8},{6,10},{8,4},{10,6},{12,0},{14,2},{16,28},{18,... | collective-permute-start | bytes 221192 | tf_op jit(solution)/shard_map/ppermute | solution.py:178
  46.6 1.1 %collective-permute-done.15.refs_1_ = bf16[48,768]{1,0:T(8,128)(2,1)S(1)} collective-permute-done((bf16[48,768]{1,0:T(8,128)(2,1)S(1)}, bf16[48,768]{1,0:T(8,128)(2,1)S(1)}, u32[]{:S(2)}, u32[]{:S(2)}) %collective-permute-start.15) | collective-permute-done | bytes 73760 | tf_op jit(solution)/shard_map/ppermute | solution.py:178
  47.7 0.9 %collective-permute-done.16.refs_2_ = bf16[48,768]{1,0:T(8,128)(2,1)S(1)} collective-permute-done((bf16[48,768]{1,0:T(8,128)(2,1)S(1)}, bf16[48,768]{1,0:T(8,128)(2,1)S(1)}, u32[]{:S(2)}, u32[]{:S(2)}) %collective-permute-start.16) | collective-permute-done | bytes 73760 | tf_op jit(solution)/shard_map/ppermute | solution.py:178
  48.7 1.8 %collective-permute-done.17.refs_3_ = bf16[48,768]{1,0:T(8,128)(2,1)S(1)} collective-permute-done((bf16[48,768]{1,0:T(8,128)(2,1)S(1)}, bf16[48,768]{1,0:T(8,128)(2,1)S(1)}, u32[]{:S(2)}, u32[]{:S(2)}) %collective-permute-start.17) | collective-permute-done | bytes 73760 | tf_op jit(solution)/shard_map/ppermute | solution.py:178
  50.5 0.7 %shard_map.40 = bf16[48,3072]{1,0:T(8,128)(2,1)} custom-call(s32[1]{0:T(128)} %bitcast.group_ref, bf16[48,768]{1,0:T(8,128)(2,1)S(1)} %get-tuple-element.33.refs_0_, bf16[48,768]{1,0:T(8,128)(2,1)S(1)} %collective-permute-done.15.refs_1_, bf16[48,768]{1,0:T(8,128)(2,1)S(1)} %collective-permute-done.16.refs_2_, ...), custom_call_target="tpu_custom_call" | custom-call | tf_op jit(solution)/shard_map/pallas_call | solution.py:152
  (8 shorter events, 0.0 us)
Async XLA Ops:
  1.4 9.6 %collective-permute-start.3 = (bf16[2,6,48,128]{3,2,1,0:T(8,128)(2,1)S(1)}, bf16[2,6,48,128]{3,2,1,0:T(8,128)(2,1)S(1)}, u32[]{:S(2)}, u32[]{:S(2)}) collective-permute-start(bf16[2,6,48,128]{3,2,1,0:T(8,128)(2,1)S(1)} %get-tuple-element.25), channel_id=1, source_target_pairs={{0,2},{2,0},{4,6},{6,4},{8,10},{10,8},{12,14},{14,12},{16,18},{18,... | collective-permute-start | bytes 442376 | tf_op jit(solution)/shard_map/ppermute | solution.py:182
  2.0 9.3 %collective-permute-start = (bf16[3,6,48,128]{3,2,1,0:T(8,128)(2,1)S(1)}, bf16[3,6,48,128]{3,2,1,0:T(8,128)(2,1)S(1)}, u32[]{:S(2)}, u32[]{:S(2)}) collective-permute-start(bf16[3,6,48,128]{3,2,1,0:T(8,128)(2,1)S(1)} %get-tuple-element.22), channel_id=1, source_target_pairs={{0,4},{2,6},{4,0},{6,2},{8,12},{10,14},{12,8},{14,10},{16,20},{18,... | collective-permute-start | bytes 663560 | tf_op jit(solution)/shard_map/ppermute | solution.py:178
  4.5 8.3 %collective-permute-start.1 = (bf16[3,6,48,128]{3,2,1,0:T(8,128)(2,1)S(1)}, bf16[3,6,48,128]{3,2,1,0:T(8,128)(2,1)S(1)}, u32[]{:S(2)}, u32[]{:S(2)}) collective-permute-start(bf16[3,6,48,128]{3,2,1,0:T(8,128)(2,1)S(1)} %get-tuple-element.23), channel_id=1, source_target_pairs={{0,8},{2,10},{4,12},{6,14},{8,0},{10,2},{12,4},{14,6},{16,24},{18,... | collective-permute-start | bytes 663560 | tf_op jit(solution)/shard_map/ppermute | solution.py:178
  6.1 21.3 %collective-permute-start.2 = (bf16[3,6,48,128]{3,2,1,0:T(8,128)(2,1)S(1)}, bf16[3,6,48,128]{3,2,1,0:T(8,128)(2,1)S(1)}, u32[]{:S(2)}, u32[]{:S(2)}) collective-permute-start(bf16[3,6,48,128]{3,2,1,0:T(8,128)(2,1)S(1)} %get-tuple-element.24), channel_id=1, source_target_pairs={{0,12},{2,14},{4,8},{6,10},{8,4},{10,6},{12,0},{14,2},{16,28},{18,... | collective-permute-start | bytes 663560 | tf_op jit(solution)/shard_map/ppermute | solution.py:178
  6.1 17.4 %collective-permute-start.7 = (bf16[2,6,48,128]{3,2,1,0:T(8,128)(2,1)S(1)}, bf16[2,6,48,128]{3,2,1,0:T(8,128)(2,1)S(1)}, u32[]{:S(2)}, u32[]{:S(2)}) collective-permute-start(bf16[2,6,48,128]{3,2,1,0:T(8,128)(2,1)S(1)} %get-tuple-element.30), channel_id=1, source_target_pairs={{0,28},{2,30},{4,24},{6,26},{8,20},{10,22},{12,16},{14,18},{16,12}... | collective-permute-start | bytes 442376 | tf_op jit(solution)/shard_map/ppermute | solution.py:178
  11.1 15.7 %collective-permute-start.8 = (bf16[2,6,48,128]{3,2,1,0:T(8,128)(2,1)S(1)}, bf16[2,6,48,128]{3,2,1,0:T(8,128)(2,1)S(1)}, u32[]{:S(2)}, u32[]{:S(2)}) collective-permute-start(bf16[2,6,48,128]{3,2,1,0:T(8,128)(2,1)S(1)} %get-tuple-element.31), channel_id=1, source_target_pairs={{0,24},{2,26},{4,28},{6,30},{8,16},{10,18},{12,20},{14,22},{16,8},... | collective-permute-start | bytes 442376 | tf_op jit(solution)/shard_map/ppermute | solution.py:178
  11.3 27.3 %collective-permute-start.4 = (bf16[3,6,48,128]{3,2,1,0:T(8,128)(2,1)S(1)}, bf16[3,6,48,128]{3,2,1,0:T(8,128)(2,1)S(1)}, u32[]{:S(2)}, u32[]{:S(2)}) collective-permute-start(bf16[3,6,48,128]{3,2,1,0:T(8,128)(2,1)S(1)} %collective-permute-done.refs_1_), channel_id=1, source_target_pairs={{0,2},{2,0},{4,6},{6,4},{8,10},{10,8},{12,14},{14,12},{16,18},{18,... | collective-permute-start | bytes 663560 | tf_op jit(solution)/shard_map/ppermute | solution.py:182
  12.8 26.3 %collective-permute-start.5 = (bf16[3,6,48,128]{3,2,1,0:T(8,128)(2,1)S(1)}, bf16[3,6,48,128]{3,2,1,0:T(8,128)(2,1)S(1)}, u32[]{:S(2)}, u32[]{:S(2)}) collective-permute-start(bf16[3,6,48,128]{3,2,1,0:T(8,128)(2,1)S(1)} %collective-permute-done.1.refs_2_), channel_id=1, source_target_pairs={{0,2},{2,0},{4,6},{6,4},{8,10},{10,8},{12,14},{14,12},{16,18},{18,... | collective-permute-start | bytes 663560 | tf_op jit(solution)/shard_map/ppermute | solution.py:182
  23.5 11.9 %collective-permute-start.9 = (bf16[2,6,48,128]{3,2,1,0:T(8,128)(2,1)S(1)}, bf16[2,6,48,128]{3,2,1,0:T(8,128)(2,1)S(1)}, u32[]{:S(2)}, u32[]{:S(2)}) collective-permute-start(bf16[2,6,48,128]{3,2,1,0:T(8,128)(2,1)S(1)} %get-tuple-element.32), channel_id=1, source_target_pairs={{0,20},{2,22},{4,16},{6,18},{8,28},{10,30},{12,24},{14,26},{16,4},... | collective-permute-start | bytes 442376 | tf_op jit(solution)/shard_map/ppermute | solution.py:178
  26.8 11.8 %collective-permute-start.10 = (bf16[2,6,48,128]{3,2,1,0:T(8,128)(2,1)S(1)}, bf16[2,6,48,128]{3,2,1,0:T(8,128)(2,1)S(1)}, u32[]{:S(2)}, u32[]{:S(2)}) collective-permute-start(bf16[2,6,48,128]{3,2,1,0:T(8,128)(2,1)S(1)} %get-tuple-element.25), channel_id=1, source_target_pairs={{0,16},{2,18},{4,20},{6,22},{8,24},{10,26},{12,28},{14,30},{16,0},... | collective-permute-start | bytes 442376 | tf_op jit(solution)/shard_map/ppermute | solution.py:178
  27.4 11.7 %collective-permute-start.6 = (bf16[3,6,48,128]{3,2,1,0:T(8,128)(2,1)S(1)}, bf16[3,6,48,128]{3,2,1,0:T(8,128)(2,1)S(1)}, u32[]{:S(2)}, u32[]{:S(2)}) collective-permute-start(bf16[3,6,48,128]{3,2,1,0:T(8,128)(2,1)S(1)} %collective-permute-done.2.refs_3_), channel_id=1, source_target_pairs={{0,2},{2,0},{4,6},{6,4},{8,10},{10,8},{12,14},{14,12},{16,18},{18,... | collective-permute-start | bytes 663560 | tf_op jit(solution)/shard_map/ppermute | solution.py:182
  35.5 5.5 %collective-permute-start.11 = (bf16[2,6,48,128]{3,2,1,0:T(8,128)(2,1)S(1)}, bf16[2,6,48,128]{3,2,1,0:T(8,128)(2,1)S(1)}, u32[]{:S(2)}, u32[]{:S(2)}) collective-permute-start(bf16[2,6,48,128]{3,2,1,0:T(8,128)(2,1)S(1)} %collective-permute-done.7.refs_4_), channel_id=1, source_target_pairs={{0,2},{2,0},{4,6},{6,4},{8,10},{10,8},{12,14},{14,12},{16,18},{18,... | collective-permute-start | bytes 442376 | tf_op jit(solution)/shard_map/ppermute | solution.py:182
  38.6 2.4 %collective-permute-start.12 = (bf16[2,6,48,128]{3,2,1,0:T(8,128)(2,1)S(1)}, bf16[2,6,48,128]{3,2,1,0:T(8,128)(2,1)S(1)}, u32[]{:S(2)}, u32[]{:S(2)}) collective-permute-start(bf16[2,6,48,128]{3,2,1,0:T(8,128)(2,1)S(1)} %collective-permute-done.8.refs_5_), channel_id=1, source_target_pairs={{0,2},{2,0},{4,6},{6,4},{8,10},{10,8},{12,14},{14,12},{16,18},{18,... | collective-permute-start | bytes 442376 | tf_op jit(solution)/shard_map/ppermute | solution.py:182
  38.6 2.4 %collective-permute-start.13 = (bf16[2,6,48,128]{3,2,1,0:T(8,128)(2,1)S(1)}, bf16[2,6,48,128]{3,2,1,0:T(8,128)(2,1)S(1)}, u32[]{:S(2)}, u32[]{:S(2)}) collective-permute-start(bf16[2,6,48,128]{3,2,1,0:T(8,128)(2,1)S(1)} %collective-permute-done.9.refs_6_), channel_id=1, source_target_pairs={{0,2},{2,0},{4,6},{6,4},{8,10},{10,8},{12,14},{14,12},{16,18},{18,... | collective-permute-start | bytes 442376 | tf_op jit(solution)/shard_map/ppermute | solution.py:182
  39.1 1.9 %collective-permute-start.14 = (bf16[2,6,48,128]{3,2,1,0:T(8,128)(2,1)S(1)}, bf16[2,6,48,128]{3,2,1,0:T(8,128)(2,1)S(1)}, u32[]{:S(2)}, u32[]{:S(2)}) collective-permute-start(bf16[2,6,48,128]{3,2,1,0:T(8,128)(2,1)S(1)} %collective-permute-done.10.refs_7_), channel_id=1, source_target_pairs={{0,2},{2,0},{4,6},{6,4},{8,10},{10,8},{12,14},{14,12},{16,18},{18,... | collective-permute-start | bytes 442376 | tf_op jit(solution)/shard_map/ppermute | solution.py:182
  43.1 4.7 %collective-permute-start.15 = (bf16[48,768]{1,0:T(8,128)(2,1)S(1)}, bf16[48,768]{1,0:T(8,128)(2,1)S(1)}, u32[]{:S(2)}, u32[]{:S(2)}) collective-permute-start(bf16[48,768]{1,0:T(8,128)(2,1)S(1)} %get-tuple-element.34), channel_id=1, source_target_pairs={{0,4},{2,6},{4,0},{6,2},{8,12},{10,14},{12,8},{14,10},{16,20},{18,... | collective-permute-start | bytes 221192 | tf_op jit(solution)/shard_map/ppermute | solution.py:178
  43.7 5.0 %collective-permute-start.16 = (bf16[48,768]{1,0:T(8,128)(2,1)S(1)}, bf16[48,768]{1,0:T(8,128)(2,1)S(1)}, u32[]{:S(2)}, u32[]{:S(2)}) collective-permute-start(bf16[48,768]{1,0:T(8,128)(2,1)S(1)} %get-tuple-element.35), channel_id=1, source_target_pairs={{0,8},{2,10},{4,12},{6,14},{8,0},{10,2},{12,4},{14,6},{16,24},{18,... | collective-permute-start | bytes 221192 | tf_op jit(solution)/shard_map/ppermute | solution.py:178
  43.7 6.8 %collective-permute-start.17 = (bf16[48,768]{1,0:T(8,128)(2,1)S(1)}, bf16[48,768]{1,0:T(8,128)(2,1)S(1)}, u32[]{:S(2)}, u32[]{:S(2)}) collective-permute-start(bf16[48,768]{1,0:T(8,128)(2,1)S(1)} %get-tuple-element.36), channel_id=1, source_target_pairs={{0,12},{2,14},{4,8},{6,10},{8,4},{10,6},{12,0},{14,2},{16,28},{18,... | collective-permute-start | bytes 221192 | tf_op jit(solution)/shard_map/ppermute | solution.py:178
